TPU v7x, 32 devices: a whole 2x2x4 slice. The times are simulated.
32 devices in a mesh: ep: 16 (over z, y, x), tp: 2 (over core).
Axes of the slice: x: 2, y: 2, z: 4, core: 2. Of those that a mesh axis runs over, the one named last changes fastest.
Arguments:
- tokens: bfloat16 [512, 6144], P('ep', 'tp'), may hold values from -6 to 6
- expert_ids: int32 [512, 8], P('ep'), may hold values from 0 to 15, all different within a row; in each aligned block of 32 rows (0 to 31, 32 to 63, ...) at most 30 rows name the same one
- gate_scores: float32 [512, 8], P('ep'), may hold values from 0.05 to 0.6
- routed_gate: bfloat16 [16, 6144, 2048], P('ep', None, 'tp'), may hold values from -0.078125 to 0.078125
- routed_up: bfloat16 [16, 6144, 2048], P('ep', None, 'tp'), may hold values from -0.078125 to 0.078125
- routed_down: bfloat16 [16, 2048, 6144], P('ep', 'tp'), may hold values from -0.1875 to 0.1875
- shared_gate: bfloat16 [6144, 2048], P(None, 'tp'), may hold values from -0.078125 to 0.078125
- shared_up: bfloat16 [6144, 2048], P(None, 'tp'), may hold values from -0.078125 to 0.078125
- shared_down: bfloat16 [2048, 6144], P('tp'), may hold values from -0.1875 to 0.1875
Outputs:
- moe_out: bfloat16 [512, 6144], P('ep', 'tp')
Inputs may be any that keep to these rules, and one draw needn't show every extreme that they name: `expert_ids`: each row names 8 different experts. Among the 32 rows of one aligned block no expert is named more than 30 times, and in some block one expert is named exactly 30 times.
All inputs are finite; a program needn't handle non-finite values.
Results may differ from a plain program's by a relative error of at most 0.019.
Values may be sent and summed in bfloat16 or wider, within the bound.
A program may use at most 128 MiB of HBM per device.

v0:
```python
import jax
import jax.numpy as jnp
from jax import lax
from jax.sharding import PartitionSpec as P


def routing(expert_ids, gate_scores, experts, capacity):
    row_count, top_count = expert_ids.shape
    entries = expert_ids.reshape(-1)
    onehot = (entries[:, None] == jnp.arange(experts, dtype=jnp.int32)[None, :]).astype(jnp.int32)
    before = jnp.cumsum(onehot, axis=0, dtype=jnp.int32) - onehot
    slot_rank = jnp.sum(before * onehot, axis=1)
    position = entries * capacity + slot_rank
    places = jnp.arange(experts * capacity, dtype=jnp.int32)[:, None] == position[None, :]
    places = places.reshape(experts * capacity, row_count, top_count).astype(jnp.float32)
    select = jnp.sum(places, axis=2).astype(jnp.bfloat16)
    combine_weights = jnp.sum(places * gate_scores[None, :, :], axis=2)
    return (select, combine_weights)


def fold_maker(w_gate, w_up, block_piece):
    return (
        jnp.dot(block_piece, w_gate, preferred_element_type=jnp.float32),
        jnp.dot(block_piece, w_up, preferred_element_type=jnp.float32),
    )


def local(
    tokens,
    expert_ids,
    gate_scores,
    routed_gate,
    routed_up,
    routed_down,
    shared_gate,
    shared_up,
    shared_down,
):
    experts = routed_gate.shape[0] * lax.axis_size("ep")
    row_count, top_count = expert_ids.shape
    capacity = min(row_count, row_count * top_count * 15 // (8 * experts))
    select, combine_weights = routing(expert_ids, gate_scores, experts, capacity)
    width_local = tokens.shape[1]
    buckets = jnp.dot(select, tokens, preferred_element_type=jnp.float32).astype(jnp.bfloat16)
    buckets = buckets.reshape(experts, capacity, width_local)
    w_gate = routed_gate[0]
    w_up = routed_up[0]
    w_down = routed_down[0]
    shared_gate_sum, shared_up_sum = fold_maker(
        shared_gate, shared_up, lax.all_gather(tokens, "tp", axis=1, tiled=True)
    )
    shared_hidden = (jax.nn.silu(shared_gate_sum) * shared_up_sum).astype(jnp.bfloat16)
    shared_partial = jnp.dot(shared_hidden, shared_down, preferred_element_type=jnp.float32).astype(
        jnp.bfloat16
    )
    shared_out = lax.psum_scatter(shared_partial, "tp", scatter_dimension=1, tiled=True).astype(
        jnp.float32
    )
    received = lax.all_to_all(buckets, "ep", split_axis=0, concat_axis=0, tiled=True)
    gate_sum, up_sum = fold_maker(w_gate, w_up, lax.all_gather(received, "tp", axis=2, tiled=True))
    hidden = (jax.nn.silu(gate_sum) * up_sum).astype(jnp.bfloat16)
    partial_value = jnp.dot(hidden, w_down, preferred_element_type=jnp.float32).astype(jnp.bfloat16)
    summed = (
        lax.psum_scatter(partial_value, "tp", scatter_dimension=2, tiled=True)
        .astype(jnp.float32)
        .astype(jnp.bfloat16)
    )
    returned = lax.all_to_all(summed, "ep", split_axis=0, concat_axis=0, tiled=True)
    flat_returned = returned.reshape(experts * capacity, width_local).astype(jnp.float32)
    routed = jnp.einsum(
        "pt,pd->td", combine_weights, flat_returned, precision=lax.Precision.HIGHEST
    )
    return (routed + shared_out).astype(jnp.bfloat16)


def solution(mesh):
    placed = (
        P("ep", "tp"),
        P("ep", None),
        P("ep", None),
        P("ep", None, "tp"),
        P("ep", None, "tp"),
        P("ep", "tp", None),
        P(None, "tp"),
        P(None, "tp"),
        P("tp", None),
    )
    return jax.shard_map(
        local, mesh=mesh, in_specs=placed, out_specs=P("ep", "tp"), check_vma=False
    )
```

profile of v0, /device:TPU:14, one launch (start us, length us, event | category | flops | bytes accessed | tf_op | source)
XLA Modules:
  0.0 247.8 jit_solution(3964499180741379840)
XLA Ops:
  6.5 0.0 all-gather.2.cloned.1.call-start
  6.5 0.8 copy.17
  7.3 0.1 eq.40
  7.4 0.1 eq.44
  7.5 0.6 reduce-window.6
  8.1 0.2 slice_reduce_fusion
  8.3 0.1 fusion.22
  8.4 0.1 reduce_sum.30
  8.5 0.8 copy.21
  9.3 1.0 convert_reduce_fusion
  10.3 3.5 %convolution_convert_fusion.1 = bf16[480,3072]{1,0:T(8,128)(2,1)} fusion(bf16[32,3072]{1,0:T(8,128)(2,1)} %param.9, bf16[480,32]{0,1:T(8,128)(2,1)S(1)} %get-tuple-element.5), kind=kOutput, calls=%fused_computation.8 | convolution fusion | flops 95846400 | bytes 3176448 | tf_op jit(solution)/shard_map/dot_general | solution.py:44
  13.8 2.9 %reshape.43 = bf16[16,30,3072]{2,1,0:T(8,128)(2,1)S(1)} reshape(bf16[480,3072]{1,0:T(8,128)(2,1)} %convolution_convert_fusion.1) | data formatting | bytes 5898240 | tf_op jit(solution)/shard_map/reshape | solution.py:45
  16.7 76.2 %all_to_all.10 = bf16[16,30,3072]{2,1,0:T(8,128)(2,1)} all-to-all(bf16[16,30,3072]{2,1,0:T(8,128)(2,1)S(1)} %reshape.43), channel_id=1, replica_groups=mesh['ep'=16,'tp'=2] {'ep'}, dimensions={0} | all-to-all | bytes 5898240 | tf_op jit(solution)/shard_map/all_to_all | solution.py:59
  92.9 0.0 all-gather.2.cloned.1.call-update
  93.0 0.0 reduce-scatter.3.cloned.1.call-start
  93.0 17.1 %all-gather.2.cloned.1.call-done = bf16[16,30,6144]{2,1,0:T(8,128)(2,1)} async-done(((bf16[16,30,3072]{2,1,0:T(8,128)(2,1)}), bf16[16,30,6144]{2,1,0:T(8,128)(2,1)}) %all-gather.2.cloned.1.call-update) | async-done | bytes 5898256 | tf_op jit(solution)/shard_map/all_gather | solution.py:60
  110.1 0.0 copy-start.1
  110.1 0.0 slice-start
  110.1 0.0 slice-start.1
  110.1 11.6 %fusion.2 = f32[16,30,1024]{2,1,0:T(8,128)S(1)} fusion(bf16[16,30,6144]{2,1,0:T(8,128)(2,1)} %all-gather.2.cloned.1.call-done, bf16[1,6144,1024]{2,1,0:T(8,128)(2,1)} %param.13), kind=kOutput, calls=%fused_computation.2 | convolution fusion | flops 6039797760 | bytes 20447232 | tf_op jit(solution)/shard_map/dot_general | solution.py:24
  121.7 0.0 copy-done.1
  121.7 0.0 slice-start.2
  121.7 10.2 %multiply_convert_fusion = bf16[16,30,1024]{2,1,0:T(8,128)(2,1)S(1)} fusion(f32[16,30,1024]{2,1,0:T(8,128)S(1)} %fusion.2, bf16[16,30,6144]{2,1,0:T(8,128)(2,1)S(1)} %copy-done.1, bf16[1,6144,1024]{2,1,0:T(8,128)(2,1)} %param.12), kind=kOutput, calls=%fused_computation.11 | convolution fusion | flops 6042746880 | bytes 21430272 | tf_op jit(solution)/shard_map/dot_general | solution.py:23
  131.9 0.0 slice-done
  132.0 0.0 slice-done.1
  132.0 0.0 slice-done.2
  132.0 8.7 %fusion.6 = bf16[16,30,6144]{2,1,0:T(8,128)(2,1)} fusion(bf16[16,30,1024]{2,1,0:T(8,128)(2,1)S(1)} %multiply_convert_fusion, bf16[1,1024,6144]{2,1,0:T(8,128)(2,1)S(1)} %bitcast.48), kind=kOutput, calls=%fused_computation.6 | convolution fusion | flops 6042746880 | bytes 19464192 | tf_op jit(solution)/shard_map/dot_general | solution.py:62
  140.7 0.0 reduce-scatter.3.cloned.1.call-update
  140.7 15.3 %reduce-scatter.3.cloned.1.call-done = bf16[16,30,3072]{2,1,0:T(8,128)(2,1)} async-done(((bf16[16,30,6144]{2,1,0:T(8,128)(2,1)}), bf16[16,30,3072]{2,1,0:T(8,128)(2,1)}) %reduce-scatter.3.cloned.1.call-update) | async-done | bytes 2949136 | tf_op jit(solution)/shard_map/reduce_scatter | solution.py:64
  156.0 7.0 %all-to-all-start.1 = ((bf16[16,30,3072]{2,1,0:T(8,128)(2,1)}), bf16[16,30,3072]{2,1,0:T(8,128)(2,1)S(1)}, u32[]{:S(2)}, u32[]{:S(2)}) async-start(bf16[16,30,3072]{2,1,0:T(8,128)(2,1)} %reduce-scatter.3.cloned.1.call-done), calls=%async_computation.2 | async-start | bytes 6291456 | tf_op jit(solution)/shard_map/all_to_all | solution.py:68
  162.9 0.0 reduce-scatter.5.cloned.1.call-start
  163.0 2.5 %all_gather.7 = bf16[32,6144]{1,0:T(8,128)(2,1)S(1)} all-gather(bf16[32,3072]{1,0:T(8,128)(2,1)} %param.9), channel_id=1, replica_groups=mesh['ep'=16,'tp'=2] {'tp'}, dimensions={1}, use_global_device_ids=true | all-gather | bytes 589824 | tf_op jit(solution)/shard_map/all_gather | solution.py:50
  165.5 7.5 %fusion.25 = f32[32,1024]{1,0:T(8,128)} fusion(bf16[32,6144]{1,0:T(8,128)(2,1)S(1)} %all_gather.7, bf16[6144,1024]{1,0:T(8,128)(2,1)} %param.15), kind=kOutput, calls=%fused_computation.35 | convolution fusion | flops 402653184 | bytes 13107200 | tf_op jit(solution)/shard_map/dot_general | solution.py:23
  173.0 13.5 %convolution_convert_fusion = bf16[32,6144]{1,0:T(8,128)(2,1)} fusion(bf16[1024,6144]{1,0:T(8,128)(2,1)} %param.17, bf16[32,6144]{1,0:T(8,128)(2,1)S(1)} %all_gather.7, bf16[6144,1024]{1,0:T(8,128)(2,1)} %param.16, f32[32,1024]{1,0:T(8,128)} %fusion.25), kind=kOutput, calls=%fused_computation.7 | convolution fusion | flops 805699584 | bytes 26083328 | tf_op jit(solution)/shard_map/dot_general | solution.py:53
  186.4 0.0 copy-start
  186.4 0.0 reduce-scatter.5.cloned.1.call-update
  186.4 48.3 %all-to-all-done.1 = bf16[16,30,3072]{2,1,0:T(8,128)(2,1)S(1)} async-done(((bf16[16,30,3072]{2,1,0:T(8,128)(2,1)}), bf16[16,30,3072]{2,1,0:T(8,128)(2,1)S(1)}, u32[]{:S(2)}, u32[]{:S(2)}) %all-to-all-start.1) | async-done | bytes 2949152 | tf_op jit(solution)/shard_map/all_to_all | solution.py:68
  234.7 2.4 reshape.44
  237.2 0.0 reduce-scatter.5.cloned.1.call-done
  237.2 0.0 copy-done
  237.2 4.1 %fusion.9 = bf16[32,3072]{1,0:T(8,128)(2,1)} fusion(f32[480,32]{0,1:T(8,128)S(1)} %copy-done, bf16[480,3072]{1,0:T(8,128)(2,1)} %reshape.44, bf16[32,3072]{1,0:T(8,128)(2,1)} %reduce-scatter.5.cloned.1.call-done), kind=kOutput, calls=%fused_computation.10 | convolution fusion | flops 566525952 | bytes 3403776 | tf_op jit(solution)/shard_map/pt,pd->td/dot_general | solution.py:70
  (5 shorter events, 0.1 us)
Async XLA Ops:
  6.5 103.6 %all-gather.2.cloned.1.call-start = ((), (), s32[]{:S(2)}) async-start(), calls=%async_computation.4 | async-start | bytes 9437184 | tf_op jit(solution)/shard_map/all_gather | solution.py:60
  93.0 63.0 %reduce-scatter.3.cloned.1.call-start = ((), (), s32[]{:S(2)}) async-start(), calls=%async_computation.5 | async-start | bytes 9437184 | tf_op jit(solution)/shard_map/reduce_scatter | solution.py:64
  110.1 11.6 %copy-start.1 = (bf16[16,30,6144]{2,1,0:T(8,128)(2,1)S(1)}, bf16[16,30,6144]{2,1,0:T(8,128)(2,1)}, u32[]{:S(2)}) copy-start(bf16[16,30,6144]{2,1,0:T(8,128)(2,1)} %all-gather.2.cloned.1.call-done) | copy-start | bytes 17694724
  110.1 21.8 %slice-start = ((s8[12582912]{0:T(1024)(128)(4,1)}), s8[4194304]{0:T(1024)(128)(4,1)S(1)}, s32[]{:S(2)}) async-start(s8[12582912]{0:T(1024)(128)(4,1)} %bitcast.47), calls=%async_computation.7 | async-start | bytes 8388608
  110.1 21.9 %slice-start.1 = ((s8[12582912]{0:T(1024)(128)(4,1)}), s8[4194304]{0:T(1024)(128)(4,1)S(1)}, s32[]{:S(2)}) async-start(s8[12582912]{0:T(1024)(128)(4,1)} %bitcast.47), calls=%async_computation.8 | async-start | bytes 8388608
  121.7 10.3 %slice-start.2 = ((s8[12582912]{0:T(1024)(128)(4,1)}), s8[4194304]{0:T(1024)(128)(4,1)S(1)}, s32[]{:S(2)}) async-start(s8[12582912]{0:T(1024)(128)(4,1)} %bitcast.47), calls=%async_computation.9 | async-start | bytes 8388608
  156.0 78.7 %all-to-all-start.1 = ((bf16[16,30,3072]{2,1,0:T(8,128)(2,1)}), bf16[16,30,3072]{2,1,0:T(8,128)(2,1)S(1)}, u32[]{:S(2)}, u32[]{:S(2)}) async-start(bf16[16,30,3072]{2,1,0:T(8,128)(2,1)} %reduce-scatter.3.cloned.1.call-done), calls=%async_computation.2 | async-start | bytes 6291456 | tf_op jit(solution)/shard_map/all_to_all | solution.py:68
  162.9 74.2 %reduce-scatter.5.cloned.1.call-start = ((), (), s32[]{:S(2)}) async-start(), calls=%async_computation.6 | async-start | bytes 589824 | tf_op jit(solution)/shard_map/reduce_scatter | solution.py:56
  186.4 50.7 %copy-start = (f32[480,32]{0,1:T(8,128)S(1)}, f32[480,32]{0,1:T(8,128)}, u32[]{:S(2)}) copy-start(f32[480,32]{0,1:T(8,128)} %get-tuple-element.6) | copy-start | bytes 184324
Sparse Core Ops, SparseCore 0:
  93.1 16.9 all-gather.1
  140.8 15.1 reduce-scatter.2
  186.6 8.8 reduce-scatter.4
where the time goes:
time: 248 us
  waiting for transfers between devices  80.7 us (33%)
  blocking collectives  78.7 us (32%)
  matrix products  59 us (24%)
  between operations  13.2 us (5%)
  local copies, waits for them, and re-layouts  7.36 us (3%)
  starting transfers between devices  7.04 us (3%)
    all_to_all x1, blocking collectives, local(): lax.all_to_all(buckets, 'ep', split_axis=0, concat_axis=0, tiled=True)  76.2 us
    all_to_all x1, waiting for transfers between devices, local(): lax.all_to_all(summed, 'ep', split_axis=0, concat_axis=0, tiled=True)  48.3 us
    dot_general x2, matrix products, fold_maker(): jnp.dot(block_piece, w_gate, preferred_element_type=jnp.float32)  17.7 us
    all_gather x1, waiting for transfers between devices, local(): lax.all_gather(received, 'tp', axis=2, tiled=True)  17.1 us
    reduce_scatter x1, waiting for transfers between devices, local(): lax.psum_scatter(partial_value, 'tp', scatter_dimension=2, tiled=True)  15.3 us
    dot_general x1, matrix products, local(): jnp.dot(shared_hidden, shared_down, preferred_element_type=jnp.float32)  13.5 us
    dot_general x1, matrix products, fold_maker(): jnp.dot(block_piece, w_up, preferred_element_type=jnp.float32)  11.6 us
    dot_general x1, matrix products, local(): jnp.dot(hidden, w_down, preferred_element_type=jnp.float32)  8.67 us
  transfers between devices with their start and end apart: 4, of which 3 were waited for; matrix products, arithmetic and copies ran while one was open for 9% of the time, Pallas kernels for 0%

commit v1 on v0

--- a/solution.py
+++ b/solution.py
@@ -25,7 +25,7 @@
     )
 
 
-def local(
+def bucketed(
     tokens,
     expert_ids,
     gate_scores,
@@ -73,6 +73,55 @@
     return (routed + shared_out).astype(jnp.bfloat16)
 
 
+def dense(
+    tokens,
+    expert_ids,
+    gate_scores,
+    routed_gate,
+    routed_up,
+    routed_down,
+    shared_gate,
+    shared_up,
+    shared_down,
+):
+    ep, tp = lax.axis_size("ep"), lax.axis_size("tp")
+    me = lax.axis_index("ep")
+    rows, width = tokens.shape
+    units = shared_gate.shape[1] // ep
+    own = jnp.arange(ep, dtype=jnp.int32)
+    scores = jnp.sum(
+        jnp.where(expert_ids[:, :, None] == own[None, None, :], gate_scores[:, :, None], 0.0), axis=1
+    )
+    scores = lax.all_gather(scores, "ep", axis=0, tiled=True)
+    weight = lax.dynamic_slice_in_dim(scores, me, 1, axis=1)
+    held = lax.all_gather(tokens, ("ep", "tp"), axis=0, tiled=False).reshape(ep, tp, rows, width)
+    features = [held[:, t].reshape(ep * rows, width) for t in range(tp)]
+    s_gate = lax.dynamic_slice_in_dim(shared_gate, me * units, units, axis=1)
+    s_up = lax.dynamic_slice_in_dim(shared_up, me * units, units, axis=1)
+    s_down = lax.dynamic_slice_in_dim(shared_down, me * units, units, axis=0)
+
+    def project(w):
+        return sum(
+            jnp.dot(
+                features[t], w[t * width : (t + 1) * width], preferred_element_type=jnp.float32
+            )
+            for t in range(tp)
+        )
+
+    hidden = (jax.nn.silu(project(routed_gate[0])) * project(routed_up[0]) * weight).astype(
+        jnp.bfloat16
+    )
+    s_hidden = (jax.nn.silu(project(s_gate)) * project(s_up)).astype(jnp.bfloat16)
+    parts = []
+    for t in range(tp):
+        cut = slice(t * width, (t + 1) * width)
+        part = jnp.dot(hidden, routed_down[0][:, cut], preferred_element_type=jnp.float32)
+        part = part + jnp.dot(s_hidden, s_down[:, cut], preferred_element_type=jnp.float32)
+        parts.append(part.astype(jnp.bfloat16).reshape(ep, 1, rows, width))
+    partial = jnp.concatenate(parts, axis=1).reshape(ep * tp, rows, width)
+    return lax.psum_scatter(partial, ("ep", "tp"), scatter_dimension=0, tiled=False)
+
+
 def solution(mesh):
     placed = (
         P("ep", "tp"),
@@ -85,6 +134,11 @@
         P(None, "tp"),
         P("tp", None),
     )
+
+    def local(*args):
+        even = args[6].shape[1] % mesh.shape["ep"] == 0
+        return (dense if even else bucketed)(*args)
+
     return jax.shard_map(
         local, mesh=mesh, in_specs=placed, out_specs=P("ep", "tp"), check_vma=False
     )

time: 248 us -> 256 us (1.032)
  waiting for transfers between devices: 80.7 us -> 157 us
  blocking collectives: 78.7 us -> 29.1 us
  matrix products: 59 us -> 42.4 us
  starting transfers between devices: 7.04 us -> 0.04 us
    reduce_scatter x2 -> x1, waiting for transfers between devices: 15.3 us -> 114 us  [dense(): lax.psum_scatter(partial, ('ep', 'tp'), scatter_dimension=0, tiled=False)]
    all_to_all x1 -> x0, blocking collectives: 76.2 us -> none  [local(): lax.all_to_all(buckets, 'ep', split_axis=0, concat_axis=0, tiled=True)]
    all_to_all x1 -> x0, waiting for transfers between devices: 48.3 us -> none  [local(): lax.all_to_all(summed, 'ep', split_axis=0, concat_axis=0, tiled=True)]
    all_gather x1, blocking collectives: 2.48 us -> 29.1 us  [dense(): scores = lax.all_gather(scores, 'ep', axis=0, tiled=True)]
    all_gather x1, waiting for transfers between devices: 17.1 us -> 42.5 us  [dense(): lax.all_gather(tokens, ('ep', 'tp'), axis=0, tiled=False)]
    dot_general x7 -> x12, matrix products: 59 us -> 42.4 us  [the longest x8 29.1 us: project(): jnp.dot(features[t], w[t * width:(t + 1) * width], preferred_element_type...]
    all_to_all x1 -> x0, starting transfers between devices: 6.96 us -> none  [local(): lax.all_to_all(summed, 'ep', split_axis=0, concat_axis=0, tiled=True)]
    reshape x2 -> x0, local copies, waits for them, and re-layouts: 5.37 us -> none  [the longest x1 2.93 us: local(): buckets = buckets.reshape(experts, capacity, width_local)]
  transfers between devices with their start and end apart: 4 -> 2, of which waited for: 3 -> 2; matrix products, arithmetic and copies ran while one was open for 9% -> 0% of each run, Pallas kernels for 0% -> 0%
where the time goes in v1:
time: 256 us; the launch traced here: 254 us
  waiting for transfers between devices  157 us (61%)
  matrix products  42.4 us (17%)
  blocking collectives  29.1 us (11%)
  between operations  13.6 us (5%)
  local copies, waits for them, and re-layouts  9.85 us (4%)
    reduce_scatter x1, waiting for transfers between devices, dense(): lax.psum_scatter(partial, ('ep', 'tp'), scatter_dimension=0, tiled=False)  114 us
    all_gather x1, waiting for transfers between devices, dense(): lax.all_gather(tokens, ('ep', 'tp'), axis=0, tiled=False)  42.5 us
    dot_general x8, matrix products, project(): jnp.dot(features[t], w[t * width:(t + 1) * width], preferred_element_type...  29.1 us
    all_gather x1, blocking collectives, dense(): scores = lax.all_gather(scores, 'ep', axis=0, tiled=True)  29.1 us
    dot_general x2, matrix products, dense(): jnp.dot(hidden, routed_down[0][:, cut], preferred_element_type=jnp.float32)  9.29 us
  transfers between devices with their start and end apart: 2, of which 2 were waited for; matrix products, arithmetic and copies ran while one was open for 0% of the time, Pallas kernels for 0%

profile of v1, /device:TPU:14, one launch (start us, length us, event | category | flops | bytes accessed | tf_op | source)
XLA Modules:
  0.0 253.8 jit_solution(11739752585782691501)
XLA Ops:
  6.5 0.0 all-gather.4.cloned.1.call-start
  6.5 0.7 all-gather.4.cloned.1.call-update
  7.3 0.0 reduce-scatter.2.cloned.1.call-start
  7.3 0.7 select_reduce_fusion
  8.0 29.1 %all-gather.1 = f32[16,32,16]{1,2,0:T(8,128)S(1)} all-gather(f32[1,32,16]{1,2,0:T(8,128)S(1)} %bitcast.58), channel_id=1, replica_groups=mesh['ep'=16,'tp'=2] {'ep'}, dimensions={0}, use_global_device_ids=true | all-gather | bytes 34816 | tf_op jit(solution)/shard_map/all_gather | solution.py:95
  37.2 0.1 reshape.25
  37.3 42.5 %all-gather.4.cloned.1.call-done = bf16[1024,3072]{1,0:T(8,128)(2,1)} async-done(((bf16[32,3072]{1,0:T(8,128)(2,1)}), bf16[1024,3072]{1,0:T(8,128)(2,1)}) %all-gather.4.cloned.1.call-update) | async-done | bytes 6291472 | tf_op jit(solution)/shard_map/all_gather | solution.py:97
  79.8 0.0 copy-start
  79.8 3.6 %fusion.33 = (bf16[16,1,32,3072]{3,2,1,0:T(8,128)(2,1)S(1)}, bf16[16,1,32,3072]{3,2,1,0:T(8,128)(2,1)S(1)}) fusion(bf16[16,2,32,3072]{3,2,1,0:T(8,128)(2,1)} %bitcast.57), kind=kLoop, calls=%fused_computation.40 | loop fusion | bytes 12582912 | tf_op jit(solution)/shard_map/slice | solution.py:98
  83.4 2.9 %copy-done = bf16[1,6144,1024]{2,1,0:T(8,128)(2,1)S(1)} copy-done((bf16[1,6144,1024]{2,1,0:T(8,128)(2,1)S(1)}, bf16[1,6144,1024]{2,1,0:T(8,128)(2,1)}, u32[]{:S(2)}) %copy-start) | copy-done | bytes 12582936
  86.3 0.0 slice-start
  86.3 0.0 slice-start.1
  86.3 3.4 %fusion.6 = f32[512,1024]{1,0:T(8,128)S(1)} fusion(bf16[512,3072]{1,0:T(8,128)(2,1)S(1)} %bitcast.50, bf16[1,6144,1024]{2,1,0:T(8,128)(2,1)S(1)} %copy-done), kind=kOutput, calls=%fused_computation.7 | convolution fusion | flops 3221225472 | bytes 11534336 | tf_op jit(solution)/shard_map/dot_general | solution.py:105
  89.7 0.0 slice-start.2
  89.7 4.7 %fusion.4 = f32[512,1024]{1,0:T(8,128)} fusion(bf16[512,3072]{1,0:T(8,128)(2,1)S(1)} %bitcast.46, bf16[1,6144,1024]{2,1,0:T(8,128)(2,1)S(1)} %copy-done), kind=kOutput, calls=%fused_computation.5 | convolution fusion | flops 3221225472 | bytes 11534336 | tf_op jit(solution)/shard_map/dot_general | solution.py:105
  94.4 0.0 slice-done
  94.4 0.0 slice-done.1
  94.4 0.0 slice-done.2
  94.4 0.0 copy-start.1
  94.5 3.4 %fusion.8 = f32[512,1024]{1,0:T(8,128)S(1)} fusion(bf16[512,3072]{1,0:T(8,128)(2,1)S(1)} %bitcast.47, bf16[1,6144,1024]{2,1,0:T(8,128)(2,1)S(1)} %bitcast.61), kind=kOutput, calls=%fused_computation.9 | convolution fusion | flops 3221225472 | bytes 11534336 | tf_op jit(solution)/shard_map/dot_general | solution.py:105
  97.9 0.0 copy-done.1
  97.9 0.0 slice-start.3
  97.9 0.0 slice-start.4
  97.9 6.8 %multiply_convert_fusion = bf16[512,1024]{1,0:T(8,128)(2,1)S(1)} fusion(f32[512,1024]{1,0:T(8,128)S(1)} %fusion.6, f32[512,1024]{1,0:T(8,128)S(1)} %copy-done.1, f32[512,1024]{1,0:T(8,128)S(1)} %fusion.8, bf16[512,3072]{1,0:T(8,128)(2,1)S(1)} %bitcast.51, bf16[1,6144,1024]{2,1,0:T(8,128)(2,1)} %param.12, f32[512]{0:T(512)S(1)} %bitcast.59), kind=kOutput, calls=%fused_computation.19 | convolution fusion | flops 3225944064 | bytes 16779264 | tf_op jit(solution)/shard_map/dot_general | solution.py:105
  104.7 0.0 slice-start.5
  104.7 5.9 %fusion = f32[512,3072]{1,0:T(8,128)S(1)} fusion(bf16[512,1024]{1,0:T(8,128)(2,1)S(1)} %multiply_convert_fusion, bf16[1024,6144]{1,0:T(8,128)(2,1)} %bitcast.62), kind=kOutput, calls=%fused_computation | convolution fusion | flops 3221225472 | bytes 13631488 | tf_op jit(solution)/shard_map/dot_general | solution.py:118
  110.6 0.0 slice-done.3
  110.6 0.0 slice-done.4
  110.6 0.0 slice-done.5
  110.6 3.4 %fusion.2 = f32[512,3072]{1,0:T(8,128)S(1)} fusion(bf16[512,1024]{1,0:T(8,128)(2,1)S(1)} %multiply_convert_fusion, bf16[1024,6144]{1,0:T(8,128)(2,1)S(1)} %bitcast.65), kind=kOutput, calls=%fused_computation.2 | convolution fusion | flops 3221225472 | bytes 13631488 | tf_op jit(solution)/shard_map/dot_general | solution.py:118
  114.1 2.7 %fusion.23 = f32[64,512]{1,0:T(8,128)S(1)} fusion(bf16[512,3072]{1,0:T(8,128)(2,1)S(1)} %bitcast.52, bf16[6144,1024]{1,0:T(8,128)(2,1)} %param.16, s32[]{:T(128)S(6)} %select_n.14), kind=kOutput, calls=%fused_computation.27 | convolution fusion | flops 201326592 | bytes 4063236 | tf_op jit(solution)/shard_map/dot_general | solution.py:105
  116.8 2.7 %fusion.26 = f32[64,512]{1,0:T(8,128)S(1)} fusion(bf16[512,3072]{1,0:T(8,128)(2,1)S(1)} %bitcast.53, bf16[6144,1024]{1,0:T(8,128)(2,1)} %param.15, s32[]{:T(128)S(6)} %select_n.14), kind=kOutput, calls=%fused_computation.30 | convolution fusion | flops 201326592 | bytes 4063236 | tf_op jit(solution)/shard_map/dot_general | solution.py:105
  119.5 2.7 %fusion.20 = f32[512,64]{0,1:T(8,128)S(1)} fusion(f32[64,512]{1,0:T(8,128)S(1)} %fusion.26, bf16[512,3072]{1,0:T(8,128)(2,1)S(1)} %bitcast.48, bf16[6144,1024]{1,0:T(8,128)(2,1)} %param.15, s32[]{:T(128)S(6)} %add.54, s32[]{:T(128)S(6)} %select_n.14), kind=kOutput, calls=%fused_computation.24 | convolution fusion | flops 201359360 | bytes 4194312 | tf_op jit(solution)/shard_map/dot_general | solution.py:105
  122.2 2.7 %fusion.21 = bf16[512,64]{0,1:T(8,128)(2,1)S(1)} fusion(f32[64,512]{1,0:T(8,128)S(1)} %fusion.23, bf16[512,3072]{1,0:T(8,128)(2,1)S(1)} %bitcast.49, bf16[6144,1024]{1,0:T(8,128)(2,1)} %param.16, s32[]{:T(128)S(6)} %add.54, s32[]{:T(128)S(6)} %select_n.14, f32[512,64]{0,1:T(8,128)S(1)} %fusion.20), kind=kOutput, calls=%fused_computation.25 | convolution fusion | flops 201555968 | bytes 4259848 | tf_op jit(solution)/shard_map/dot_general | solution.py:105
  124.9 2.0 add_convert_fusion
  126.9 2.0 add_convert_fusion.1
  128.9 0.6 pad_maximum_fusion
  129.5 3.2 %copy.24 = bf16[16,2,32,3072]{3,2,1,0:T(8,128)(2,1)} copy(bf16[16,2,32,3072]{3,2,0,1:T(8,128)(2,1)S(1)} %pad_maximum_fusion) | data formatting | bytes 12582912 | tf_op jit(solution)/shard_map/concatenate | solution.py:121
  132.7 0.0 reduce-scatter.2.cloned.1.call-update
  132.7 114.3 %reduce-scatter.2.cloned.1.call-done = bf16[1,32,3072]{2,1,0:T(8,128)(2,1)} async-done(((bf16[32,32,3072]{2,1,0:T(8,128)(2,1)}), bf16[1,32,3072]{2,1,0:T(8,128)(2,1)}) %reduce-scatter.2.cloned.1.call-update) | async-done | bytes 196624 | tf_op jit(solution)/shard_map/reduce_scatter | solution.py:122
  (4 shorter events, 0.1 us)
Async XLA Ops:
  6.5 73.3 %all-gather.4.cloned.1.call-start = ((), (), s32[]{:S(2)}) async-start(), calls=%async_computation.2 | async-start | bytes 6488064 | tf_op jit(solution)/shard_map/all_gather | solution.py:97
  7.3 239.7 %reduce-scatter.2.cloned.1.call-start = ((), (), s32[]{:S(2)}) async-start(), calls=%async_computation.1 | async-start | bytes 6488064 | tf_op jit(solution)/shard_map/reduce_scatter | solution.py:122
  79.8 6.4 %copy-start = (bf16[1,6144,1024]{2,1,0:T(8,128)(2,1)S(1)}, bf16[1,6144,1024]{2,1,0:T(8,128)(2,1)}, u32[]{:S(2)}) copy-start(bf16[1,6144,1024]{2,1,0:T(8,128)(2,1)} %param.13) | copy-start | bytes 37748740
  86.3 8.2 %slice-start = ((s8[12582912]{0:T(1024)(128)(4,1)}), s8[4194304]{0:T(1024)(128)(4,1)S(1)}, s32[]{:S(2)}) async-start(s8[12582912]{0:T(1024)(128)(4,1)} %bitcast.60), calls=%async_computation.3 | async-start | bytes 8388608
  86.3 8.2 %slice-start.1 = ((s8[12582912]{0:T(1024)(128)(4,1)}), s8[4194304]{0:T(1024)(128)(4,1)S(1)}, s32[]{:S(2)}) async-start(s8[12582912]{0:T(1024)(128)(4,1)} %bitcast.60), calls=%async_computation.4 | async-start | bytes 8388608
  89.7 4.8 %slice-start.2 = ((s8[12582912]{0:T(1024)(128)(4,1)}), s8[4194304]{0:T(1024)(128)(4,1)S(1)}, s32[]{:S(2)}) async-start(s8[12582912]{0:T(1024)(128)(4,1)} %bitcast.60), calls=%async_computation.5 | async-start | bytes 8388608
  94.4 3.4 %copy-start.1 = (f32[512,1024]{1,0:T(8,128)S(1)}, f32[512,1024]{1,0:T(8,128)}, u32[]{:S(2)}) copy-start(f32[512,1024]{1,0:T(8,128)} %fusion.4) | copy-start | bytes 6291460
  97.9 12.7 %slice-start.3 = ((s8[12582912]{0:T(1024)(128)(4,1)}), s8[4194304]{0:T(1024)(128)(4,1)S(1)}, s32[]{:S(2)}) async-start(s8[12582912]{0:T(1024)(128)(4,1)} %bitcast.63), calls=%async_computation.6 | async-start | bytes 8388608
  97.9 12.7 %slice-start.4 = ((s8[12582912]{0:T(1024)(128)(4,1)}), s8[4194304]{0:T(1024)(128)(4,1)S(1)}, s32[]{:S(2)}) async-start(s8[12582912]{0:T(1024)(128)(4,1)} %bitcast.63), calls=%async_computation.7 | async-start | bytes 8388608
  104.7 5.9 %slice-start.5 = ((s8[12582912]{0:T(1024)(128)(4,1)}), s8[4194304]{0:T(1024)(128)(4,1)S(1)}, s32[]{:S(2)}) async-start(s8[12582912]{0:T(1024)(128)(4,1)} %bitcast.63), calls=%async_computation.8 | async-start | bytes 8388608
Sparse Core Ops, SparseCore 0:
  10.2 69.5 all-gather.3
  132.8 114.0 reduce-scatter.1

commit v2 on v0

--- a/solution.py
+++ b/solution.py
@@ -1,6 +1,10 @@
+import functools
+
 import jax
 import jax.numpy as jnp
 from jax import lax
+from jax.experimental import pallas as pl
+from jax.experimental.pallas import tpu as pltpu
 from jax.sharding import PartitionSpec as P
 
 
@@ -25,7 +29,7 @@
     )
 
 
-def local(
+def bucketed(
     tokens,
     expert_ids,
     gate_scores,
@@ -73,6 +77,415 @@
     return (routed + shared_out).astype(jnp.bfloat16)
 
 
+LANES = 128
+TILE = 256
+QUAD = 4
+MESH = pl.DeviceIdType.MESH
+
+
+def layer_kernel(
+    ep,
+    x_ref,
+    gate_hbm,
+    up_hbm,
+    down_hbm,
+    s_in_hbm,
+    s_down_hbm,
+    out_ref,
+    xbuf,
+    w_gate,
+    w_up,
+    w_down,
+    w_shared,
+    hidden,
+    mine,
+    other,
+    other_in,
+    last_in,
+    line_in,
+    first_in,
+    w_sem,
+    own_sem,
+    gather_send,
+    gather_recv,
+    core_send,
+    core_recv,
+    last_send,
+    last_recv,
+    line_send,
+    line_recv,
+    first_send,
+    first_recv,
+):
+    depth = ep // QUAD
+    rows, width = out_ref.shape
+    units = w_gate.shape[1]
+    e, c = lax.axis_index("ep"), lax.axis_index("tp")
+    z, y, x = e // QUAD, (e // 2) % 2, e % 2
+    flip_x, flip_y = 1 - 2 * x, 1 - 2 * y
+    f = x * (1 - c) + y * c
+    l = y * (1 - c) + x * c
+
+    def block(zz, ff, ll):
+        return zz * QUAD + (1 - c) * (2 * ll + ff) + c * (2 * ff + ll)
+
+    sibling = (e, 1 - c)
+    first = (e + (1 - c) * flip_x + c * 2 * flip_y, c)
+    last = (e + c * flip_x + (1 - c) * 2 * flip_y, c)
+    above = (e + QUAD, c)
+    below = (e - QUAD, c)
+    has_above, has_below = z < depth - 1, z > 0
+
+    loads = [
+        pltpu.make_async_copy(gate_hbm, w_gate, w_sem.at[0]),
+        pltpu.make_async_copy(up_hbm, w_up, w_sem.at[1]),
+        pltpu.make_async_copy(s_in_hbm, w_shared, w_sem.at[2]),
+        pltpu.make_async_copy(down_hbm, w_down.at[pl.ds(0, units)], w_sem.at[3]),
+        pltpu.make_async_copy(
+            s_down_hbm, w_down.at[pl.ds(units, s_down_hbm.shape[0])], w_sem.at[4]
+        ),
+    ]
+    own = pltpu.make_async_copy(x_ref, xbuf.at[c, e], own_sem)
+    own.start()
+    for load in loads:
+        load.start()
+
+    barrier = pltpu.get_barrier_semaphore()
+    for peer in (sibling, first, last):
+        pl.semaphore_signal(barrier, inc=1, device_id=peer, device_id_type=MESH)
+
+    @pl.when(has_above)
+    def _():
+        pl.semaphore_signal(barrier, inc=1, device_id=above, device_id_type=MESH)
+
+    @pl.when(has_below)
+    def _():
+        pl.semaphore_signal(barrier, inc=1, device_id=below, device_id_type=MESH)
+
+    pl.semaphore_wait(
+        barrier, 3 + jnp.where(has_above, 1, 0) + jnp.where(has_below, 1, 0)
+    )
+    own.wait()
+
+    def gather_copy(kind, b, half, peer):
+        return pltpu.make_async_remote_copy(
+            src_ref=xbuf.at[half, b],
+            dst_ref=xbuf.at[half, b],
+            send_sem=gather_send.at[kind, b],
+            recv_sem=gather_recv.at[half, b],
+            device_id=peer,
+            device_id_type=MESH,
+        )
+
+    TO_FIRST, TO_LAST, TO_ABOVE, TO_BELOW, TO_CORE = range(5)
+
+    def arrived(b, half):
+        gather_copy(TO_CORE, b, half, sibling).wait_recv()
+
+    def up_down(b, go_above, go_below):
+        @pl.when(go_above)
+        def _():
+            gather_copy(TO_ABOVE, b, c, above).start()
+
+        @pl.when(go_below)
+        def _():
+            gather_copy(TO_BELOW, b, c, below).start()
+
+    gather_copy(TO_FIRST, e, c, first).start()
+    up_down(e, has_above, has_below)
+    gather_copy(TO_LAST, e, c, last).start()
+    gather_copy(TO_CORE, e, c, sibling).start()
+    partner = block(z, 1 - f, l)
+    arrived(partner, c)
+    up_down(partner, has_above, has_below)
+    gather_copy(TO_LAST, partner, c, last).start()
+    gather_copy(TO_CORE, partner, c, sibling).start()
+
+    def from_last(zz):
+        for ff in range(2):
+            b = block(zz, ff, 1 - l)
+            arrived(b, c)
+            gather_copy(TO_CORE, b, c, sibling).start()
+
+    for d in range(1, depth):
+        for ff in (f, 1 - f):
+
+            @pl.when(z - d >= 0)
+            def _():
+                b = block(z - d, ff, l)
+                arrived(b, c)
+                up_down(b, has_above, False)
+                gather_copy(TO_LAST, b, c, last).start()
+                gather_copy(TO_CORE, b, c, sibling).start()
+
+            @pl.when(z + d < depth)
+            def _():
+                b = block(z + d, ff, l)
+                arrived(b, c)
+                up_down(b, False, has_below)
+                gather_copy(TO_LAST, b, c, last).start()
+                gather_copy(TO_CORE, b, c, sibling).start()
+
+        if d == 1:
+            from_last(z)
+        else:
+            pl.when(z - d + 1 >= 0)(lambda: from_last(z - d + 1))
+            pl.when(z + d - 1 < depth)(lambda: from_last(z + d - 1))
+    pl.when(z - depth + 1 >= 0)(lambda: from_last(z - depth + 1))
+    pl.when(z + depth - 1 < depth)(lambda: from_last(z + depth - 1))
+
+    @pl.loop(0, ep)
+    def _(b):
+        arrived(b, 1 - c)
+
+    for load in loads[:3]:
+        load.wait()
+
+    tokens = ep * rows
+    tag = xbuf[0, :, :, pl.ds(width, LANES)].reshape(tokens, LANES).astype(jnp.float32)
+    lane = lax.broadcasted_iota(jnp.int32, (tokens, LANES), 1)
+    chosen = (lane == e) | (lane == e + ep) | (lane == e + 2 * ep)
+    weight = jnp.sum(jnp.where(chosen, tag, 0.0), axis=1, keepdims=True)
+
+    def project(w_ref, start):
+        total = None
+        for half in range(2):
+            part = jnp.dot(
+                xbuf[half, :, :, pl.ds(0, width)].reshape(tokens, width),
+                w_ref[pl.ds(half * width, width), pl.ds(start, TILE)],
+                preferred_element_type=jnp.float32,
+            )
+            total = part if total is None else total + part
+        return total
+
+    @pl.loop(0, units // TILE)
+    def _(j):
+        start = pl.multiple_of(j * TILE, TILE)
+        g = project(w_gate, start)
+        u = project(w_up, start)
+        h = g / (1.0 + jnp.exp(-g)) * u * weight
+        hidden[:, pl.ds(start, TILE)] = h.astype(jnp.bfloat16)
+
+    both = project(w_shared, 0)
+    g, u = both[:, :LANES], both[:, LANES:]
+    hidden[:, pl.ds(units, LANES)] = (g / (1.0 + jnp.exp(-g)) * u).astype(jnp.bfloat16)
+
+    for load in loads[3:]:
+        load.wait()
+
+    def contract(half, target):
+        @pl.loop(0, width // TILE)
+        def _(j):
+            start = pl.multiple_of(j * TILE, TILE)
+            column = pl.multiple_of(half * width + j * TILE, TILE)
+            part = jnp.dot(
+                hidden[...], w_down[:, pl.ds(column, TILE)], preferred_element_type=jnp.float32
+            )
+            target[:, :, pl.ds(start, TILE)] = part.astype(jnp.bfloat16).reshape(ep, rows, TILE)
+
+    contract(1 - c, other)
+    to_core = pltpu.make_async_remote_copy(
+        src_ref=other,
+        dst_ref=other_in,
+        send_sem=core_send,
+        recv_sem=core_recv,
+        device_id=sibling,
+        device_id_type=MESH,
+    )
+    to_core.start()
+    contract(c, mine)
+    to_core.wait()
+
+    def add(b, ref, *at):
+        mine[b] = (mine[b].astype(jnp.float32) + ref[at].astype(jnp.float32)).astype(jnp.bfloat16)
+
+    order = []
+    for zz in range(depth):
+        near = sorted(range(depth), key=lambda p: (-abs(p - zz), p))
+        order.append(near)
+
+    def pick(k):
+        p = jnp.int32(0)
+        for zz in range(depth):
+            p = jnp.where(z == zz, order[zz][k], p)
+        return p
+
+    def last_copy(p, ff, b):
+        return pltpu.make_async_remote_copy(
+            src_ref=mine.at[b],
+            dst_ref=last_in.at[p, ff],
+            send_sem=last_send.at[p, ff],
+            recv_sem=last_recv.at[p, ff],
+            device_id=last,
+            device_id_type=MESH,
+        )
+
+    def line_copy(p, ff, b, slot, peer):
+        return pltpu.make_async_remote_copy(
+            src_ref=mine.at[b],
+            dst_ref=line_in.at[slot, ff],
+            send_sem=line_send.at[p, ff],
+            recv_sem=line_recv.at[slot, ff],
+            device_id=peer,
+            device_id_type=MESH,
+        )
+
+    for k in range(depth):
+        p = pick(k)
+        for ff in range(2):
+            b = block(p, ff, 1 - l)
+            add(b, other_in, b)
+            last_copy(p, ff, b).start()
+
+    home = block(z, 1 - f, l)
+    to_first = pltpu.make_async_remote_copy(
+        src_ref=mine.at[home],
+        dst_ref=first_in,
+        send_sem=first_send,
+        recv_sem=first_recv,
+        device_id=first,
+        device_id_type=MESH,
+    )
+    for k in range(depth):
+        p = pick(k)
+        for ff in (1 - f, f):
+            b = block(p, ff, l)
+            add(b, other_in, b)
+            last_copy(p, ff, b).wait_recv()
+            add(b, last_in, p, ff)
+
+            @pl.when((p >= z) & has_below)
+            def _():
+                line_copy(p, ff, b, p, above).wait_recv()
+                add(b, line_in, p, ff)
+
+            @pl.when((p <= z) & has_above)
+            def _():
+                slot = jnp.where(p == z, depth, p)
+                line_copy(p, ff, b, slot, below).wait_recv()
+                add(b, line_in, slot, ff)
+
+            @pl.when(p > z)
+            def _():
+                line_copy(p, ff, b, p, above).start()
+
+            @pl.when(p < z)
+            def _():
+                slot = jnp.where(p == z - 1, depth, p)
+                line_copy(p, ff, b, slot, below).start()
+
+        if k == depth - 1:
+            to_first.start()
+
+    to_first.wait()
+    out_ref[...] = (mine[e].astype(jnp.float32) + first_in[...].astype(jnp.float32)).astype(
+        jnp.bfloat16
+    )
+
+    for p in range(depth):
+        for ff in range(2):
+            last_copy(p, ff, block(p, ff, 1 - l)).wait_send()
+
+            @pl.when(p != z)
+            def _():
+                line_copy(p, ff, block(p, ff, l), p, above).wait_send()
+
+    gather_copy(TO_FIRST, e, c, first).wait_send()
+    for zz in range(depth):
+        for ff in range(2):
+            b = block(zz, ff, l)
+            gather_copy(TO_LAST, b, c, last).wait_send()
+            pl.when((zz <= z) & has_above)(
+                lambda: gather_copy(TO_ABOVE, b, c, above).wait_send()
+            )
+            pl.when((zz >= z) & has_below)(
+                lambda: gather_copy(TO_BELOW, b, c, below).wait_send()
+            )
+
+    @pl.loop(0, ep)
+    def _(b):
+        gather_copy(TO_CORE, b, c, sibling).wait_send()
+
+
+def dense(
+    tokens,
+    expert_ids,
+    gate_scores,
+    routed_gate,
+    routed_up,
+    routed_down,
+    shared_gate,
+    shared_up,
+    shared_down,
+):
+    ep = lax.axis_size("ep")
+    me = lax.axis_index("ep")
+    rows, width = tokens.shape
+    depth = ep // QUAD
+    features, units = routed_gate.shape[1:]
+    share = shared_gate.shape[1] // ep
+    spare = LANES - share
+    own = jnp.arange(ep, dtype=jnp.int32)
+    scores = jnp.sum(
+        jnp.where(expert_ids[:, :, None] == own[None, None, :], gate_scores[:, :, None], 0.0), axis=1
+    )
+    high = lax.reduce_precision(scores, 8, 7)
+    middle = lax.reduce_precision(scores - high, 8, 7)
+    low = scores - high - middle
+    tag = jnp.concatenate([high, middle, low], axis=1).astype(jnp.bfloat16)
+    tagged = jnp.concatenate(
+        [tokens, jnp.pad(tag, ((0, 0), (0, LANES - tag.shape[1])))], axis=1
+    )
+    s_gate = lax.dynamic_slice_in_dim(shared_gate, me * share, share, axis=1)
+    s_up = lax.dynamic_slice_in_dim(shared_up, me * share, share, axis=1)
+    s_in = jnp.concatenate(
+        [jnp.pad(s_gate, ((0, 0), (0, spare))), jnp.pad(s_up, ((0, 0), (0, spare)))], axis=1
+    )
+    s_down = jnp.pad(
+        lax.dynamic_slice_in_dim(shared_down, me * share, share, axis=0), ((0, spare), (0, 0))
+    )
+    vmem = pl.BlockSpec(memory_space=pltpu.VMEM)
+    far = pl.BlockSpec(memory_space=pl.ANY)
+    half = (rows, width)
+    dtype = tokens.dtype
+    dma = pltpu.SemaphoreType.DMA
+    return pl.pallas_call(
+        functools.partial(layer_kernel, ep),
+        out_shape=jax.ShapeDtypeStruct(half, dtype),
+        in_specs=[vmem] + [far] * 5,
+        out_specs=vmem,
+        scratch_shapes=[
+            pltpu.VMEM((2, ep, rows, width + LANES), dtype),
+            pltpu.VMEM((features, units), dtype),
+            pltpu.VMEM((features, units), dtype),
+            pltpu.VMEM((units + LANES, features), dtype),
+            pltpu.VMEM((features, TILE), dtype),
+            pltpu.VMEM((ep * rows, units + LANES), dtype),
+            pltpu.VMEM((ep,) + half, dtype),
+            pltpu.VMEM((ep,) + half, dtype),
+            pltpu.VMEM((ep,) + half, dtype),
+            pltpu.VMEM((depth, 2) + half, dtype),
+            pltpu.VMEM((depth + 1, 2) + half, dtype),
+            pltpu.VMEM(half, dtype),
+            dma((5,)),
+            dma,
+            dma((5, ep)),
+            dma((2, ep)),
+            dma,
+            dma,
+            dma((depth, 2)),
+            dma((depth, 2)),
+            dma((depth, 2)),
+            dma((depth + 1, 2)),
+            dma,
+            dma,
+        ],
+        compiler_params=pltpu.CompilerParams(
+            collective_id=0, has_side_effects=True, vmem_limit_bytes=67043328
+        ),
+    )(tagged, routed_gate[0], routed_up[0], routed_down[0], s_in, s_down)
+
+
 def solution(mesh):
     placed = (
         P("ep", "tp"),
@@ -85,6 +498,12 @@
         P(None, "tp"),
         P("tp", None),
     )
+
+    def local(*args):
+        ep, tp = mesh.shape["ep"], mesh.shape["tp"]
+        fits = tp == 2 and ep == QUAD * QUAD and args[6].shape[1] % ep == 0
+        return (dense if fits else bucketed)(*args)
+
     return jax.shard_map(
         local, mesh=mesh, in_specs=placed, out_specs=P("ep", "tp"), check_vma=False
     )

time: 248 us -> 118 us (0.48)
  the two profiles are of different devices: /device:TPU:14 before, /device:TPU:26 now
where the time goes in v2:
time: 118 us
  Pallas kernels  108 us (92%)
  local copies, waits for them, and re-layouts  7.02 us (6%)
  other arithmetic  2.78 us (2%)
    pallas_call x1, Pallas kernels, dense(): pl.pallas_call(functools.partial(layer_kernel, ep), out_shape=jax.ShapeDt...  108 us
    dynamic_slice x1, local copies, waits for them, and re-layouts, dense(): s_up = lax.dynamic_slice_in_dim(shared_up, me * share, share, axis=1)  2.79 us

profile of v2, /device:TPU:26, one launch (start us, length us, event | category | flops | bytes accessed | tf_op | source)
XLA Modules:
  0.0 118.2 jit_solution(6924416533954859287)
XLA Ops:
  0.0 2.8 %constant_dynamic-slice_fusion.1 = (bf16[6144,64]{1,0:T(8,128)(2,1)S(1)}, bf16[6144,64]{1,0:T(8,128)(2,1)S(1)}) fusion(bf16[6144,1024]{1,0:T(8,128)(2,1)} %param.16, s32[]{:T(128)S(6)} %select_n.10, bf16[6144,1024]{1,0:T(8,128)(2,1)} %param.15), kind=kLoop, calls=%fused_computation.18 | loop fusion | bytes 3145732 | tf_op jit(solution)/shard_map/dynamic_slice | solution.py:440
  2.8 0.0 copy-start.1
  2.8 0.0 copy-start.2
  2.8 0.0 copy-start
  2.8 2.0 %fusion.2.s_in_hbm = bf16[6144,256]{1,0:T(8,128)(2,1)} fusion(bf16[6144,64]{1,0:T(8,128)(2,1)S(1)} %get-tuple-element.8, bf16[6144,64]{1,0:T(8,128)(2,1)S(1)} %get-tuple-element.9), kind=kLoop, calls=%fused_computation.4 | loop fusion | flops 12582912 | bytes 4718592 | tf_op jit(solution)/shard_map/concatenate | solution.py:441
  4.8 0.0 copy-done.1
  4.8 0.0 copy-done.2
  4.8 0.1 copy.14
  4.9 0.1 copy.15
  5.0 0.1 fusion.8
  5.1 0.0 copy-done
  5.1 0.7 pad_maximum_fusion.x_ref
  5.8 1.2 %constant_dynamic-slice_fusion = bf16[64,6144]{1,0:T(8,128)(2,1)S(1)} fusion(bf16[1024,6144]{1,0:T(8,128)(2,1)} %param.17, s32[]{:T(128)S(6)} %select_n.10), kind=kLoop, calls=%fused_computation.17 | loop fusion | bytes 1572868 | tf_op jit(solution)/shard_map/dynamic_slice | solution.py:445
  7.0 1.3 %pad.18.s_down_hbm = bf16[128,6144]{1,0:T(8,128)(2,1)} pad(bf16[64,6144]{1,0:T(8,128)(2,1)S(1)} %constant_dynamic-slice_fusion, bf16[]{:T(256)} %constant.4.clone.1), padding=0_64x0_0 | pad | bytes 2359298 | tf_op jit(solution)/shard_map/jit(_pad)/pad | solution.py:444
  8.2 108.3 %shard_map.91 = bf16[32,3072]{1,0:T(8,128)(2,1)} custom-call(bf16[32,3200]{1,0:T(8,128)(2,1)} %pad_maximum_fusion.x_ref, bf16[6144,1024]{1,0:T(8,128)(2,1)} %bitcast.3, bf16[6144,1024]{1,0:T(8,128)(2,1)} %bitcast.4, bf16[1024,6144]{1,0:T(8,128)(2,1)} %bitcast.5, bf16[6144,256]{1,0:T(8,128)(2,1)} %fusion.2.s_in_hbm, bf16[128,6144]{1,0:T(8,128)(2,1)} %pad.18.s_down_hbm), custom_call_target="tpu_custom_call" | custom-call | tf_op jit(solution)/shard_map/pallas_call | solution.py:452
  116.5 1.6 %copy.18 = bf16[32,3072]{1,0:T(8,128)(2,1)} copy(bf16[32,3072]{1,0:T(8,128)(2,1)} %shard_map.91) | data formatting | bytes 393216
  (3 shorter events, 0.0 us)
Async XLA Ops:
  2.8 2.0 %copy-start.1 = (f32[32,8]{0,1:T(8,128)S(1)}, f32[32,8]{0,1:T(8,128)}, u32[]{:S(2)}) copy-start(f32[32,8]{0,1:T(8,128)} %param.11) | copy-start | bytes 3076
  2.8 2.0 %copy-start.2 = (s32[32,8]{0,1:T(8,128)S(1)}, s32[32,8]{0,1:T(8,128)}, u32[]{:S(2)}) copy-start(s32[32,8]{0,1:T(8,128)} %param.10) | copy-start | bytes 3076
  2.8 2.3 %copy-start = (bf16[32,3072]{1,0:T(8,128)(2,1)S(1)}, bf16[32,3072]{1,0:T(8,128)(2,1)}, u32[]{:S(2)}) copy-start(bf16[32,3072]{1,0:T(8,128)(2,1)} %param.9) | copy-start | bytes 589828
